TPU v7x, 512 devices: a whole 4x8x8 slice. The times are simulated.
512 devices in a mesh: row: 32 (over y_hi, z, core), col: 16 (over x, y_lo).
Axes of the slice: x: 4, y: 8 (y_hi: 2, y_lo: 4; y = y_hi * 4 + y_lo), z: 8, core: 2. Of those that a mesh axis runs over, the one named last changes fastest.
Arguments:
- embedding: bfloat16 [1024, 128], P('col'), may hold values from -6 to 6
- dilation: int32 [2], replicated, may hold values from 1 to 4, as said below
- kernel: bfloat16 [3, 3, 48, 128], replicated, may hold values from -0.1875 to 0.1875
- kernel_bias: float32 [48], replicated, may hold values from -3 to 3
- mixing: bfloat16 [5, 48], replicated, may hold values from -0.875 to 0.875
- mixing_bias: float32 [5], replicated, may hold values from -3 to 3
- cotangent: bfloat16 [5, 1024, 1024], P(None, 'row', 'col'), may hold values from -0.375 to 0.375
Outputs:
- contact: float32 [5, 1024, 1024], P(None, 'row', 'col')
- embedding_grad: float32 [1024, 128], P('col')
- kernel_grad: float32 [3, 3, 48, 128], replicated
Inputs may be any that keep to these rules, and one draw needn't show every extreme that they name: `dilation`: the larger of the two rates is exactly 4.
All inputs are finite; a program needn't handle non-finite values.
Results may differ from a plain program's by a relative error of at most 0.019.
The roundings to bfloat16 on the way count: a program that leaves them out, or rounds other values in their place, can miss the bound.
Values may be sent and summed in bfloat16 or wider, within the bound.
A program may use at most 64 MiB of HBM per device.

v0:
```python
import jax
import jax.numpy as jnp
from jax import lax
from jax.sharding import PartitionSpec as P

DMAX = 4


def copy_for_each(value, axis):
    peers = lax.axis_size(axis)
    return lax.all_to_all(
        jnp.broadcast_to(value[None], (peers, *value.shape)), axis, 0, 0, tiled=True
    )


def laid_out(tiles, dim):
    shape = list(tiles.shape[1:])
    shape[dim] *= tiles.shape[0]
    return jnp.moveaxis(tiles, 0, dim).reshape(shape)


def gather_directly(value, axis, dim):
    tiles = copy_for_each(value, axis)
    return laid_out(tiles, dim)


def tap_list():
    return [(tap_row, tap_col) for tap_row in (-1, 0, 1) for tap_col in (-1, 0, 1)]


def narrow(values):
    return values.astype(jnp.bfloat16)


def add_into(target, position, update):
    current = lax.dynamic_slice_in_dim(target, position, update.shape[0], 0)
    return lax.dynamic_update_slice_in_dim(target, current + update, position, 0)


def per_device(embedding, dilation, kernel, kernel_bias, mixing, mixing_bias, cotangent):
    highest = lax.Precision.HIGHEST
    row_rate = dilation[0]
    col_rate = dilation[1]
    margin = DMAX
    channels = embedding.shape[1]
    filters = kernel.shape[2]
    row_count = cotangent.shape[1]
    col_count = cotangent.shape[2]
    col_devices = lax.axis_size("col")
    bins_total = col_count * col_devices
    row_index = lax.axis_index("row")
    col_index = lax.axis_index("col")
    row_start = row_index * row_count
    col_start = col_index * col_count
    every_bin = gather_directly(embedding, "col", 0)
    padded = jnp.pad(every_bin, ((margin, margin), (0, 0)))
    row_values = lax.dynamic_slice_in_dim(padded, row_start, row_count + 2 * margin, 0)
    col_values = lax.dynamic_slice_in_dim(padded, col_start, col_count + 2 * margin, 0)
    row_places = row_start - margin + jnp.arange(row_count + 2 * margin, dtype=jnp.int32)
    col_places = col_start - margin + jnp.arange(col_count + 2 * margin, dtype=jnp.int32)
    row_inside = ((row_places >= 0) & (row_places < bins_total)).astype(jnp.float32)
    col_inside = ((col_places >= 0) & (col_places < bins_total)).astype(jnp.float32)
    pairs = narrow(
        0.5
        * (row_values.astype(jnp.float32)[:, None, :] + col_values.astype(jnp.float32)[None, :, :])
    )
    keep_mask = (row_inside[:, None] * col_inside[None, :]).astype(jnp.bfloat16)
    pairs = pairs * keep_mask[:, :, None]
    zero_index = jnp.zeros((), jnp.int32)

    def slicer(tap_row, tap_col, mirrored):
        if mirrored:
            first_at, second_at = (margin + tap_col * col_rate, margin + tap_row * row_rate)
        else:
            first_at, second_at = (margin + tap_row * row_rate, margin + tap_col * col_rate)
        return lax.dynamic_slice(
            pairs, (first_at, second_at, zero_index), (row_count, col_count, channels)
        )

    def convolve(mirrored):
        running = jnp.zeros((filters, row_count, col_count), jnp.float32)
        for tap_row, tap_col in tap_list():
            tap_piece = slicer(tap_row, tap_col, mirrored)
            running = running + jnp.einsum(
                "ijc,fc->fij",
                tap_piece,
                kernel[tap_row + 1, tap_col + 1],
                preferred_element_type=jnp.float32,
            )
        return running + kernel_bias[:, None, None]

    direct = convolve(False)
    mirror = convolve(True)
    direct_act = narrow(jax.nn.relu(direct))
    mirror_act = narrow(jax.nn.relu(mirror))

    def mix_map(activation):
        return (
            jnp.einsum("tf,fij->tij", mixing, activation, preferred_element_type=jnp.float32)
            + mixing_bias[:, None, None]
        )

    contact = 0.5 * mix_map(direct_act) + 0.5 * mix_map(mirror_act)
    guide_grad = narrow(
        0.5 * jnp.einsum("tf,tij->fij", mixing, cotangent, preferred_element_type=jnp.float32)
    )
    grad_direct = jnp.where(direct > 0, guide_grad, jnp.zeros_like(guide_grad))
    grad_mirror = jnp.where(mirror > 0, guide_grad, jnp.zeros_like(guide_grad))
    updates = []
    for tap_row, tap_col in tap_list():
        tap_term = jnp.einsum(
            "fij,ijc->fc",
            grad_direct,
            slicer(tap_row, tap_col, False),
            preferred_element_type=jnp.float32,
        )
        tap_term = tap_term + jnp.einsum(
            "fij,ijc->fc",
            grad_mirror,
            slicer(tap_row, tap_col, True),
            preferred_element_type=jnp.float32,
        )
        updates.append(tap_term)
    kernel_terms = jnp.stack(updates).reshape(3, 3, filters, channels)
    kernel_grad = lax.psum(kernel_terms.astype(jnp.bfloat16), ("row", "col")).astype(jnp.float32)

    def col_mask(shift):
        return lax.dynamic_slice_in_dim(col_inside, margin + shift, col_count, 0).astype(
            jnp.bfloat16
        )

    def row_mask(shift):
        return lax.dynamic_slice_in_dim(row_inside, margin + shift, row_count, 0).astype(
            jnp.bfloat16
        )

    direct_rows = [
        jnp.einsum(
            "fij,j->fi",
            grad_direct,
            col_mask(tap_step * col_rate),
            preferred_element_type=jnp.float32,
        )
        for tap_step in (-1, 0, 1)
    ]
    direct_cols = [
        jnp.einsum(
            "fij,i->fj",
            grad_direct,
            row_mask(tap_step * row_rate),
            preferred_element_type=jnp.float32,
        )
        for tap_step in (-1, 0, 1)
    ]
    mirror_rows = [
        jnp.einsum(
            "fij,j->fi",
            grad_mirror,
            col_mask(tap_step * row_rate),
            preferred_element_type=jnp.float32,
        )
        for tap_step in (-1, 0, 1)
    ]
    mirror_cols = [
        jnp.einsum(
            "fij,i->fj",
            grad_mirror,
            row_mask(tap_step * col_rate),
            preferred_element_type=jnp.float32,
        )
        for tap_step in (-1, 0, 1)
    ]
    row_grad = jnp.zeros((row_count + 2 * margin, channels), jnp.float32)
    col_grad = jnp.zeros((col_count + 2 * margin, channels), jnp.float32)
    for tap_row, tap_col in tap_list():
        tap_weight = kernel[tap_row + 1, tap_col + 1].astype(jnp.float32)
        row_grad = add_into(
            row_grad,
            margin + tap_row * row_rate,
            jnp.einsum("fi,fc->ic", direct_rows[tap_col + 1], tap_weight, precision=highest),
        )
        row_grad = add_into(
            row_grad,
            margin + tap_col * col_rate,
            jnp.einsum("fi,fc->ic", mirror_rows[tap_row + 1], tap_weight, precision=highest),
        )
        col_grad = add_into(
            col_grad,
            margin + tap_col * col_rate,
            jnp.einsum("fj,fc->jc", direct_cols[tap_row + 1], tap_weight, precision=highest),
        )
        col_grad = add_into(
            col_grad,
            margin + tap_row * row_rate,
            jnp.einsum("fj,fc->jc", mirror_cols[tap_col + 1], tap_weight, precision=highest),
        )
    empty_term = jnp.zeros((bins_total + 2 * margin, channels), jnp.float32)
    row_part = lax.dynamic_update_slice_in_dim(empty_term, row_grad, row_start, 0)
    col_part = lax.dynamic_update_slice_in_dim(empty_term, col_grad, col_start, 0)
    whole_term = (
        0.5 * row_part[margin : margin + bins_total] + 0.5 * col_part[margin : margin + bins_total]
    )
    whole_grad = lax.psum(whole_term.astype(jnp.bfloat16), ("row", "col")).astype(jnp.float32)
    embedding_grad = lax.dynamic_slice_in_dim(whole_grad, col_start, col_count, 0)
    return (contact, embedding_grad, kernel_grad)


def solution(mesh):
    return jax.shard_map(
        per_device,
        mesh=mesh,
        in_specs=(P("col", None), P(), P(), P(), P(), P(), P(None, "row", "col")),
        out_specs=(P(None, "row", "col"), P("col", None), P()),
        check_vma=False,
    )
```

profile of v0, /device:TPU:1, one launch (start us, length us, event | category | flops | bytes accessed | tf_op | source)
XLA Modules:
  0.0 350.1 jit_solution(6438566248406176946)
XLA Ops:
  7.2 1.5 broadcast_in_dim.8
  8.7 8.0 %all-to-all-start = ((bf16[16,64,128]{2,1,0:T(8,128)(2,1)}), bf16[16,64,128]{2,1,0:T(8,128)(2,1)S(1)}, u32[]{:S(2)}, u32[]{:S(2)}) async-start(bf16[16,64,128]{2,1,0:T(8,128)(2,1)} %broadcast_in_dim.8), calls=%async_computation | async-start | bytes 524288 | tf_op jit(solution)/shard_map/all_to_all | solution.py:11
  16.7 0.6 fusion.307
  22.6 2.0 all-to-all-done
  24.7 0.4 fusion.44
  25.2 0.6 fusion.83
  25.8 0.6 fusion.70
  26.4 0.6 convolution_add_fusion.6
  27.0 0.6 convolution_add_fusion.5
  27.7 0.6 fusion.1
  28.3 0.6 convolution_add_fusion.3
  28.9 0.6 convolution_add_fusion.2
  29.6 0.6 convolution_add_fusion.1
  30.2 0.6 fusion.79
  30.8 0.6 convolution_add_fusion.13
  31.4 0.6 convolution_add_fusion.12
  32.1 0.6 fusion.3
  32.7 0.6 convolution_add_fusion.10
  33.3 0.6 convolution_add_fusion.9
  34.0 0.6 convolution_add_fusion.8
  34.6 0.6 fusion
  35.2 0.6 fusion.2
  35.9 0.4 bitcast_select_fusion
  36.3 0.9 convolution_bitcast_fusion.16
  37.3 0.9 convolution_bitcast_fusion.14
  38.2 0.9 convolution_bitcast_fusion.12
  39.1 0.9 convolution_bitcast_fusion.10
  40.0 0.9 convolution_bitcast_fusion.8
  41.0 0.9 convolution_bitcast_fusion.6
  42.9 0.5 fusion.279
  43.3 0.5 fusion.281
  43.9 0.5 fusion.273
  44.4 0.5 fusion.277
  44.9 0.5 fusion.275
  45.6 0.4 dynamic_update_slice.114
  48.7 0.5 fusion.271
  62.9 0.3 fusion.29
  63.8 0.3 fusion.33
  64.2 0.3 fusion.35
  64.5 0.4 copy-done.3
  65.2 0.3 fusion.39
  65.6 0.3 fusion.41
  65.9 0.3 fusion.43
  66.4 0.8 fusion.46
  67.4 0.7 copy.11
  68.1 272.3 %all-reduce.4.cloned.1.call-done = (bf16[1024,128]{1,0:T(8,128)(2,1)}, bf16[3,3,48,128]{3,2,1,0:T(8,128)(2,1)}) async-done(((bf16[1024,128]{1,0:T(8,128)(2,1)}, bf16[3,3,48,128]{3,2,1,0:T(8,128)(2,1)}), (bf16[1024,128]{1,0:T(8,128)(2,1)}, bf16[3,3,48,128]{3,2,1,0:T(8,128)(2,1)})) %all-reduce.4.cloned.1.call-update) | async-done | bytes 372752 | tf_op jit(solution)/shard_map/psum | solution.py:203
  340.3 1.6 convert_element_type.111
  341.9 1.3 dynamic-slice_convert_fusion
  (125 shorter events, 18.5 us)
Async XLA Ops:
  7.2 28.7 %copy-start = (bf16[5,32,64]{2,1,0:T(8,128)(2,1)S(1)}, bf16[5,32,64]{2,1,0:T(8,128)(2,1)}, u32[]{:S(2)}) copy-start(bf16[5,32,64]{2,1,0:T(8,128)(2,1)} %param.13) | copy-start | bytes 61444
  7.2 9.6 %copy-start.11 = (s32[2]{0:T(128)S(1)}, s32[2]{0:T(128)}, u32[]{:S(2)}) copy-start(s32[2]{0:T(128)} %param.8) | copy-start | bytes 28
  8.7 16.0 %all-to-all-start = ((bf16[16,64,128]{2,1,0:T(8,128)(2,1)}), bf16[16,64,128]{2,1,0:T(8,128)(2,1)S(1)}, u32[]{:S(2)}, u32[]{:S(2)}) async-start(bf16[16,64,128]{2,1,0:T(8,128)(2,1)} %broadcast_in_dim.8), calls=%async_computation | async-start | bytes 524288 | tf_op jit(solution)/shard_map/all_to_all | solution.py:11
  16.7 8.5 %copy-start.1 = (bf16[3,3,48,128]{3,2,1,0:T(8,128)(2,1)S(1)}, bf16[3,3,48,128]{3,2,1,0:T(8,128)(2,1)}, u32[]{:S(2)}) copy-start(bf16[3,3,48,128]{3,2,1,0:T(8,128)(2,1)} %param.9) | copy-start | bytes 331780
  16.7 323.7 %all-reduce.4.cloned.1.call-start = ((), (), s32[]{:S(2)}) async-start(), calls=%async_computation.1 | async-start | bytes 745472 | tf_op jit(solution)/shard_map/psum | solution.py:203
  34.0 0.7 copy-start.9
  35.2 0.7 copy-start.8
  51.4 3.4 copy-start.7
  58.0 4.7 %copy-start.10 = (f32[5]{0:T(128)S(1)}, f32[5]{0:T(128)}, u32[]{:S(2)}) copy-start(f32[5]{0:T(128)} %param.12) | copy-start | bytes 64
  60.7 2.2 copy-start.6
  62.7 0.7 copy-start.5
  62.9 0.9 copy-start.4
  63.4 0.7 copy-start.12
  64.2 0.7 copy-start.3
  66.2 1.0 copy-start.2
Sparse Core Ops, SparseCore 0:
  67.3 272.9 all-reduce.3
where the time goes:
time: 351 us; the launch traced here: 350 us
  waiting for transfers between devices  274 us (78%)
  matrix products  31.4 us (9%)
  between operations  20.1 us (6%)
  local copies, waits for them, and re-layouts  11.9 us (3%)
  starting transfers between devices  8.02 us (2%)
  other arithmetic  4.34 us (1%)
    psum x1, waiting for transfers between devices, per_device(): lax.psum(whole_term.astype(jnp.bfloat16), ('row', 'col'))  272 us
    dot_general x17, matrix products, convolve(): jnp.einsum('ijc,fc->fij', tap_piece, kernel[tap_row + 1, tap_col + 1], pr...  10.5 us
    dynamic_update_slice x36, local copies, waits for them, and re-layouts, add_into(): lax.dynamic_update_slice_in_dim(target, current + update, position, 0)  8.29 us
    all_to_all x1, starting transfers between devices, copy_for_each(): lax.all_to_all(jnp.broadcast_to(value[None], (peers, *value.shape)), axis...  7.98 us
  transfers between devices with their start and end apart: 2, of which 2 were waited for; matrix products, arithmetic and copies ran while one was open for 0% of the time, Pallas kernels for 0%

commit v1 on v0

v1 whole, which is shorter than its diff:
```python
import functools

import jax
import jax.numpy as jnp
from jax import lax
from jax.experimental import pallas as pl
from jax.experimental.pallas import tpu as pltpu
from jax.sharding import PartitionSpec as P

MESH = pl.DeviceIdType.MESH
DMAX = 4
TILE = 16
LANES = 128
MIRROR = 64
TAPS = [(a, b) for a in range(3) for b in range(3)]
VM = pl.BlockSpec(memory_space=pltpu.VMEM)
SM = pl.BlockSpec(memory_space=pltpu.SMEM)


def f32(value):
    return value.astype(jnp.float32)


def b16(value):
    return value.astype(jnp.bfloat16)


def dot(a, b, dims):
    return lax.dot_general(a, b, (dims, ((), ())), preferred_element_type=jnp.float32)


def load_weights(kern, bias, mix, wconv, wall, bias_row, mix_rows):
    filters = kern.shape[2]
    wconv[...] = jnp.zeros_like(wconv)
    wall[...] = jnp.zeros_like(wall)
    bias_row[...] = jnp.zeros_like(bias_row)
    mix_rows[...] = jnp.zeros_like(mix_rows)
    for at in (0, MIRROR):
        bias_row[:, at : at + filters] = bias[...]
        mix_rows[0 : mix.shape[0], at : at + filters] = f32(mix[...])
    for n, (a, b) in enumerate(TAPS):
        tap = kern[a, b]
        wconv[0:filters, n * LANES : (n + 1) * LANES] = tap
        wconv[MIRROR : MIRROR + filters, (9 + n) * LANES : (10 + n) * LANES] = tap
        wall[b * LANES : b * LANES + filters, a * LANES : (a + 1) * LANES] = tap
        wall[a * LANES + MIRROR : a * LANES + MIRROR + filters, (3 + b) * LANES : (4 + b) * LANES] = tap


def compute(
    dil, erow, ecol, cot, mixb, contact, send,
    wconv, wall, bias_row, mix_rows,
    er, ec, xr, xc, mr, mc, cotf, lhs, sums, sums_c, prow, pcol,
    row_index, col_index, bins, half, tiles_per_owner, owners,
):
    rows = contact.shape[1]
    cols = contact.shape[2]
    row_rate = dil[0]
    col_rate = dil[1]
    shifts = [-row_rate, 0, row_rate, -col_rate, 0, col_rate]
    row_start = row_index * rows
    col_start = col_index * cols

    er[...] = 0.5 * f32(erow[...])
    ec[...] = 0.5 * f32(ecol[...])
    lane_r = lax.broadcasted_iota(jnp.int32, (rows, LANES), 1)
    lane_c = lax.broadcasted_iota(jnp.int32, (cols, LANES), 1)
    row_at = lax.broadcasted_iota(jnp.int32, (rows, LANES), 0) + row_start
    col_at = lax.broadcasted_iota(jnp.int32, (cols, LANES), 0) + col_start

    def inside(place):
        return jnp.where((place >= 0) & (place < bins), 1.0, 0.0)

    for q, shift in enumerate(shifts):
        xr[q] = er[pl.ds(TILE + shift, rows), :]
        xc[q] = b16(ec[pl.ds(TILE + shift, cols), :])
        mr[q] = inside(row_at + shift)
        mc[q] = b16(inside(col_at + shift))
    sum_rm = [
        inside(row_at + jnp.where(lane_r < MIRROR, t * row_rate, t * col_rate)) for t in (-1, 1)
    ]
    sum_cm = [
        inside(col_at + jnp.where(lane_c < MIRROR, t * col_rate, t * row_rate)) for t in (-1, 1)
    ]
    for t in range(2):
        mr[6 + t] = sum_rm[t]
    cotf[...] = f32(cot[...])
    sums_c[...] = jnp.zeros_like(sums_c)
    mix16 = b16(mix_rows[...])

    group = 8

    @pl.loop(0, rows // group)
    def _(chunk):
        base = chunk * group
        for ii in range(group):
            i = base + ii
            row16 = [b16(jnp.broadcast_to(xr[q, pl.ds(i, 1), :], (TILE, LANES))) for q in range(6)]
            rmask = [b16(jnp.broadcast_to(mr[q, pl.ds(i, 1), :], (TILE, LANES))) for q in range(6)]
            for n in range(18):
                a, b = TAPS[n % 9]
                p, q = (a, 3 + b) if n < 9 else (3 + b, a)
                for s in range(cols // TILE):
                    value = (row16[p] + xc[q, s * TILE : (s + 1) * TILE, :]) * mc[
                        q, s * TILE : (s + 1) * TILE, :
                    ]
                    lhs[ii * cols + s * TILE : ii * cols + (s + 1) * TILE, n * LANES : (n + 1) * LANES] = (
                        value * rmask[p]
                    )
        conv = dot(lhs[...], wconv[...], ((1,), (1,))) + bias_row[...]
        on = conv > 0
        act = b16(jnp.maximum(conv, 0.0))
        mixed = 0.5 * dot(mix16, act, ((1,), (1,)))
        guide = []
        for ii in range(group):
            piece = b16(cotf[:, base + ii, :])
            guide.append(dot(piece, mix16[0:8], ((0,), (0,))))
        guide = f32(b16(0.5 * jnp.concatenate(guide, axis=0)))
        grad = jnp.where(on, guide, 0.0)
        row_sums = [[], [], []]
        maps = []
        for ii in range(group):
            i = base + ii
            g = grad[ii * cols : (ii + 1) * cols]
            maps.append(mixed[0:5, ii * cols : (ii + 1) * cols] + mixb[...])
            for t in range(3):
                gr = g if t == 1 else g * sum_cm[t // 2]
                row_sums[t].append(jnp.sum(gr, axis=0, keepdims=True))
                gc = g if t == 1 else g * jnp.broadcast_to(mr[6 + t // 2, pl.ds(i, 1), :], g.shape)
                sums_c[:, t * LANES : (t + 1) * LANES] += gc
        at = pl.multiple_of(base, group)
        contact[:, pl.ds(at, group), :] = jnp.stack(maps, axis=1)
        for t in range(3):
            sums[pl.ds(at, group), t * LANES : (t + 1) * LANES] = jnp.concatenate(row_sums[t], axis=0)

    for t in range(3):
        block = sums_c[:, t * LANES : (t + 1) * LANES]
        sums[rows : rows + cols, t * LANES : (t + 1) * LANES] = pltpu.roll(block, MIRROR, 1)
    stacked = b16(sums[...])
    emb = 0.5 * dot(stacked, wall[...], ((1,), (0,)))
    prow[...] = jnp.zeros_like(prow)
    pcol[...] = jnp.zeros_like(pcol)
    for q in range(6):
        part = emb[:, q * LANES : (q + 1) * LANES]
        prow[q, 24 : 24 + rows] = part[0:rows]
        pcol[q, 24 : 24 + cols] = part[rows : rows + cols]
    row_grad = sum(prow[q, pl.ds(8 - shifts[q], rows + 2 * TILE), :] for q in range(6))
    col_grad = sum(pcol[q, pl.ds(8 - shifts[q], cols + 2 * TILE), :] for q in range(6))

    kernel_tiles = tiles_per_owner * owners
    x = [jnp.concatenate([b16(xr[q]), xc[q]], axis=0) for q in range(6)]
    wide = dot(stacked, jnp.concatenate(x, axis=1), ((0,), (0,)))
    filters = 48
    pieces = []
    for a, b in TAPS:
        tap = (
            wide[b * LANES : b * LANES + filters, a * LANES : (a + 1) * LANES]
            + wide[a * LANES + MIRROR : a * LANES + MIRROR + filters, (3 + b) * LANES : (4 + b) * LANES]
        )
        pieces += [tap[s * TILE : (s + 1) * TILE] for s in range(filters // TILE)]
    zero = jnp.zeros((TILE, LANES), jnp.bfloat16)
    for k in range(2 * kernel_tiles):
        send[k % 2, k // 2] = b16(pieces[k]) if k < len(pieces) else zero
    for k in range(6):
        send[k // 3, kernel_tiles + k % 3] = b16(col_grad[k * TILE : (k + 1) * TILE])
        send[k // 3, kernel_tiles + 3 + k % 3] = zero
    for k in range(4):
        value = b16(row_grad[k * TILE : (k + 1) * TILE])

        @pl.when(half == 0)
        def _():
            send[k // 3, kernel_tiles + 3 + k % 3] = value

        @pl.when(half == 1)
        def _():
            send[(k + 2) // 3, kernel_tiles + 3 + (k + 2) % 3] = value


def compute_kernel(owners, tiles_per_owner, bins, dil, erow, ecol, kern, bias, mix, mixb, cot, contact, send, *scratch):
    row_index = lax.axis_index("row")
    col_index = lax.axis_index("col")
    load_weights(kern, bias, mix, *scratch[:4])
    compute(
        dil, erow, ecol, cot, mixb, contact, send, *scratch,
        row_index, col_index, bins, lax.rem(row_index, 2), tiles_per_owner, owners,
    )


def compute_scratch(rows, cols, channels):
    return [
        pltpu.VMEM((LANES, 18 * LANES), jnp.bfloat16),
        pltpu.VMEM((3 * LANES, 6 * LANES), jnp.bfloat16),
        pltpu.VMEM((1, LANES), jnp.float32),
        pltpu.VMEM((8, LANES), jnp.float32),
        pltpu.VMEM((rows + 2 * TILE, LANES), jnp.float32),
        pltpu.VMEM((cols + 2 * TILE, LANES), jnp.float32),
        pltpu.VMEM((6, rows, LANES), jnp.float32),
        pltpu.VMEM((6, cols, LANES), jnp.bfloat16),
        pltpu.VMEM((8, rows, LANES), jnp.float32),
        pltpu.VMEM((6, cols, LANES), jnp.bfloat16),
        pltpu.VMEM((8, rows, cols), jnp.float32),
        pltpu.VMEM((8 * cols, 18 * LANES), jnp.bfloat16),
        pltpu.VMEM((rows + cols, 3 * LANES), jnp.float32),
        pltpu.VMEM((cols, 3 * LANES), jnp.float32),
        pltpu.VMEM((6, rows + 48, LANES), jnp.float32),
        pltpu.VMEM((6, cols + 48, LANES), jnp.float32),
    ]


class Place:
    def __init__(self, n_row, n_col):
        self.n_col = n_col
        self.n_z = n_row // 4
        self.row = lax.axis_index("row")
        self.col = lax.axis_index("col")
        self.half = lax.rem(self.row, 2)
        self.chip = self.row // 2
        self.z = lax.rem(self.chip, self.n_z)
        self.partner = self.row + 1 - 2 * self.half
        self.far = lax.rem(self.row + n_row // 2, n_row)

    def z_peer(self, z):
        return self.row + 2 * (z - self.z)


def enter(place, barrier):
    count = 0

    def greet(row, col):
        pl.semaphore_signal(barrier, inc=1, device_id=(row, col), device_id_type=MESH)

    greet(place.partner, place.col)
    greet(place.far, place.col)
    count += 2
    for d in range(1, place.n_z):
        greet(place.z_peer(lax.rem(place.z + d, place.n_z)), place.col)
        count += 1
    for d in range(1, place.n_col):
        greet(place.row, lax.rem(place.col + d, place.n_col))
        count += 1
    for d in (1, place.n_col - 1):
        greet(place.partner, lax.rem(place.col + d, place.n_col))
        count += 1
    return count


def remote(src, dst, send_sem, recv_sem, row, col):
    return pltpu.make_async_remote_copy(
        src_ref=src, dst_ref=dst, send_sem=send_sem, recv_sem=recv_sem, device_id=(row, col), device_id_type=MESH
    )


def total(ref, count):
    value = f32(ref[0])
    for k in range(1, count):
        value = value + f32(ref[k])
    return value


def reduce_all(
    place, owners, per_owner, send, emb_out, kernel_out,
    core_in, own, r_kernel, r_row, p_kernel, p_emb, y_kernel, y_emb,
    z_kernel, z_emb, full, emb_all, margins,
    core_s, kern_s, row_s, y_s, zk_s, ze_s, ag_s, agc_s, fin_s,
):
    n_col, n_z = place.n_col, place.n_z
    row, col, half = place.row, place.col, place.half
    kt = per_owner * owners

    swap = remote(send.at[1 - half], core_in, core_s.at[0], core_s.at[1], place.partner, col)
    swap.start()
    swap.wait()
    own[...] = b16(f32(send[half]) + f32(core_in[...]))

    def kernel_copy(src, dst):
        return remote(
            own.at[pl.ds(dst * per_owner, per_owner)],
            r_kernel.at[src],
            kern_s.at[0, dst],
            kern_s.at[1, src],
            row,
            dst,
        )

    for dst in range(owners):

        @pl.when(dst != col)
        def _():
            kernel_copy(col, dst).start()

    def row_copy(src):
        return remote(own.at[pl.ds(kt + 3, 3)], r_row.at[src], row_s.at[n_col], row_s.at[src], row, place.chip)

    @pl.when(col != place.chip)
    def _():
        row_copy(col).start()

    def far_copy(n, src, dst):
        return remote(src, dst, y_s.at[0, n], y_s.at[1, n], place.far, col)

    def z_copy(sems, buf, src, dst):
        return remote(buf.at[src], buf.at[src], sems.at[0, dst], sems.at[1, src], place.z_peer(dst), col)

    @pl.when(col < owners)
    def _():
        r_kernel[col] = own[pl.ds(col * per_owner, per_owner)]
        for src in range(n_col):

            @pl.when(src != col)
            def _():
                kernel_copy(src, col).wait_recv()

        p_kernel[...] = b16(total(r_kernel, n_col))
        far_copy(0, p_kernel, y_kernel).start()

    mine = f32(own[kt : kt + 3])
    p_emb[...] = b16(mine)

    @pl.when(col == place.chip)
    def _():
        r_row[col] = own[kt + 3 : kt + 6]
        for src in range(n_col):

            @pl.when(src != col)
            def _():
                row_copy(src).wait_recv()

        p_emb[...] = b16(mine + total(r_row, n_col))

    far_copy(1, p_emb, y_emb).start()

    @pl.when(col < owners)
    def _():
        far_copy(0, p_kernel, y_kernel).wait()
        z_kernel[place.z] = b16(f32(p_kernel[...]) + f32(y_kernel[...]))
        for dst in range(n_z):

            @pl.when(dst != place.z)
            def _():
                z_copy(zk_s, z_kernel, place.z, dst).start()

    far_copy(1, p_emb, y_emb).wait()
    z_emb[place.z] = b16(f32(p_emb[...]) + f32(y_emb[...]))
    for dst in range(n_z):

        @pl.when(dst != place.z)
        def _():
            z_copy(ze_s, z_emb, place.z, dst).start()

    def gather_copy(src, dst):
        return remote(full.at[half, src], full.at[half, src], ag_s.at[0, dst], ag_s.at[1, src], row, dst)

    @pl.when(col < owners)
    def _():
        for src in range(n_z):

            @pl.when(src != place.z)
            def _():
                z_copy(zk_s, z_kernel, src, place.z).wait_recv()

        full[half, col] = b16(total(z_kernel, n_z))
        for dst in range(n_col):

            @pl.when(dst != col)
            def _():
                gather_copy(col, dst).start()

    for src in range(n_z):

        @pl.when(src != place.z)
        def _():
            z_copy(ze_s, z_emb, src, place.z).wait_recv()

    emb_all[half] = b16(total(z_emb, n_z))
    emb_swap = remote(emb_all.at[half], emb_all.at[half], fin_s.at[0, 0], fin_s.at[1, 0], place.partner, col)
    emb_swap.start()
    to = col - 1 + 2 * half
    exists = (to >= 0) & (to < n_col)
    came = col + 1 - 2 * half
    came_ok = (came >= 0) & (came < n_col)
    other = col - 1 + 2 * half
    other_ok = (other >= 0) & (other < n_col)

    def margin_copy(n, device_row):
        return remote(
            emb_all.at[half, 2 * half], margins.at[half], fin_s.at[0, 1 + n], fin_s.at[1, 1 + n], device_row, to
        )

    def margin_in(n, slot):
        return remote(
            emb_all.at[half, 2 * half], margins.at[slot], fin_s.at[0, 1 + n], fin_s.at[1, 1 + n], row, col
        )

    @pl.when(exists)
    def _():
        margin_copy(0, row).start()
        margin_copy(1, place.partner).start()

    emb_swap.wait()

    @pl.when(came_ok)
    def _():
        margin_in(0, half).wait_recv()

    @pl.when(other_ok)
    def _():
        margin_in(1, 1 - half).wait_recv()

    main = [f32(emb_all[0, 1]), f32(emb_all[0, 2]), f32(emb_all[1, 0]), f32(emb_all[1, 1])]
    emb_out[0:TILE] = main[0] + f32(margins[1])
    emb_out[TILE : 2 * TILE] = main[1]
    emb_out[2 * TILE : 3 * TILE] = main[2]
    emb_out[3 * TILE : 4 * TILE] = main[3] + f32(margins[0])

    for src in range(owners):

        @pl.when(src != col)
        def _():
            gather_copy(src, col).wait_recv()

    share = remote(full.at[half], full.at[half], agc_s.at[0], agc_s.at[1], place.partner, col)
    share.start()
    share.wait()
    count = kernel_out.shape[0]
    for k in range(count):
        kernel_out[k] = f32(full[k % 2, k // (2 * per_owner), (k // 2) % per_owner])

    for dst in range(owners):

        @pl.when(dst != col)
        def _():
            kernel_copy(col, dst).wait_send()

    @pl.when(col != place.chip)
    def _():
        row_copy(col).wait_send()

    for dst in range(n_z):

        @pl.when((dst != place.z) & (col < owners))
        def _():
            z_copy(zk_s, z_kernel, place.z, dst).wait_send()

        @pl.when(dst != place.z)
        def _():
            z_copy(ze_s, z_emb, place.z, dst).wait_send()

    @pl.when(col < owners)
    def _():
        for dst in range(n_col):

            @pl.when(dst != col)
            def _():
                gather_copy(col, dst).wait_send()

    @pl.when(exists)
    def _():
        margin_copy(0, row).wait_send()
        margin_copy(1, place.partner).wait_send()


def reduce_kernel(n_row, n_col, owners, per_owner, send, emb_out, kernel_out, *scratch):
    place = Place(n_row, n_col)
    margins = scratch[12]
    margins[...] = jnp.zeros_like(margins)
    barrier = pltpu.get_barrier_semaphore()
    pl.semaphore_wait(barrier, enter(place, barrier))
    reduce_all(place, owners, per_owner, send, emb_out, kernel_out, *scratch)


def reduce_scratch(n_row, n_col, owners, per_owner):
    n_z = n_row // 4
    kt = owners * per_owner

    def tiles(*lead):
        return pltpu.VMEM((*lead, TILE, LANES), jnp.bfloat16)

    return [
        tiles(kt + 6), tiles(kt + 6), tiles(n_col, per_owner), tiles(n_col, 3),
        tiles(per_owner), tiles(3), tiles(per_owner), tiles(3),
        tiles(n_z, per_owner), tiles(n_z, 3), tiles(2, owners, per_owner), tiles(2, 3), tiles(2),
        pltpu.SemaphoreType.DMA((2,)),
        pltpu.SemaphoreType.DMA((2, n_col)),
        pltpu.SemaphoreType.DMA((n_col + 1,)),
        pltpu.SemaphoreType.DMA((2, 2)),
        pltpu.SemaphoreType.DMA((2, n_z)),
        pltpu.SemaphoreType.DMA((2, n_z)),
        pltpu.SemaphoreType.DMA((2, n_col)),
        pltpu.SemaphoreType.DMA((2,)),
        pltpu.SemaphoreType.DMA((2, 3)),
    ]


def per_device(n_row, n_col, embedding, dilation, kernel, kernel_bias, mixing, mixing_bias, cotangent):
    channels = embedding.shape[1]
    filters = kernel.shape[2]
    maps, rows, cols = cotangent.shape
    bins = cols * n_col
    count = 9 * filters // TILE
    per_owner = -(-count // (2 * n_col))
    owners = -(-count // (2 * per_owner))
    row_start = lax.axis_index("row") * rows
    col_start = lax.axis_index("col") * cols
    tiles = lax.all_to_all(
        jnp.broadcast_to(embedding[None], (n_col, *embedding.shape)), "col", 0, 0, tiled=True
    ).reshape(bins, channels)
    padded = jnp.pad(tiles, ((TILE, TILE), (0, 0)))
    erow = lax.dynamic_slice_in_dim(padded, row_start, rows + 2 * TILE, 0)
    ecol = lax.dynamic_slice_in_dim(padded, col_start, cols + 2 * TILE, 0)
    cot8 = jnp.pad(cotangent, ((0, 8 - maps), (0, 0), (0, 0)))
    contact, send = pl.pallas_call(
        functools.partial(compute_kernel, owners, per_owner, bins),
        out_shape=[
            jax.ShapeDtypeStruct((maps, rows, cols), jnp.float32),
            jax.ShapeDtypeStruct((2, owners * per_owner + 6, TILE, LANES), jnp.bfloat16),
        ],
        in_specs=[SM, VM, VM, VM, VM, VM, VM, VM],
        out_specs=[VM, VM],
        scratch_shapes=compute_scratch(rows, cols, channels),
    )(dilation, erow, ecol, kernel, kernel_bias[None], mixing, mixing_bias[:, None], cot8)
    emb, grad = pl.pallas_call(
        functools.partial(reduce_kernel, n_row, n_col, owners, per_owner),
        out_shape=[
            jax.ShapeDtypeStruct((cols, channels), jnp.float32),
            jax.ShapeDtypeStruct((count, TILE, channels), jnp.float32),
        ],
        in_specs=[VM],
        out_specs=[VM, VM],
        scratch_shapes=reduce_scratch(n_row, n_col, owners, per_owner),
        compiler_params=pltpu.CompilerParams(collective_id=0, has_side_effects=True),
    )(send)
    return contact, emb, grad.reshape(3, 3, filters, channels)


def solution(mesh):
    return jax.shard_map(
        functools.partial(per_device, mesh.shape["row"], mesh.shape["col"]),
        mesh=mesh,
        in_specs=(P("col", None), P(), P(), P(), P(), P(), P(None, "row", "col")),
        out_specs=(P(None, "row", "col"), P("col", None), P()),
        check_vma=False,
    )
```

time: 351 us -> 67.7 us (0.19)
  waiting for transfers between devices: 274 us -> 6.01 us
  Pallas kernels: 0 us -> 44.8 us
  matrix products: 31.4 us -> 0 us
  between operations: 20.1 us -> 0.67 us
  other arithmetic: 4.34 us -> 0 us
  local copies, waits for them, and re-layouts: 11.9 us -> 7.68 us
    psum x1 -> x0, waiting for transfers between devices: 272 us -> none  [per_device(): lax.psum(whole_term.astype(jnp.bfloat16), ('row', 'col'))]
    pallas_call x0 -> x2, Pallas kernels: none -> 44.8 us  [the longest x1 37.7 us: per_device(): pl.pallas_call(functools.partial(reduce_kernel, n_row, n_col, owners, per...]
    dot_general x86 -> x0, matrix products: 31.4 us -> none  [the longest x17 10.5 us: convolve(): jnp.einsum('ijc,fc->fij', tap_piece, kernel[tap_row + 1, tap_col + 1], pr...]
    dynamic_update_slice x38 -> x0, local copies, waits for them, and re-layouts: 8.31 us -> none  [the longest x36 8.29 us: add_into(): lax.dynamic_update_slice_in_dim(target, current + update, position, 0)]
    all_to_all x1, waiting for transfers between devices: 2 us -> 6.01 us  [per_device(): lax.all_to_all(jnp.broadcast_to(embedding[None], (n_col, *embedding.shape...]
    convert_element_type x8 -> x0, other arithmetic: 3.88 us -> none  [the longest x1 1.6 us: per_device(): lax.psum(kernel_terms.astype(jnp.bfloat16), ('row', 'col'))]
  transfers between devices with their start and end apart: 2 -> 1, of which waited for: 2 -> 1; matrix products, arithmetic and copies ran while one was open for 0% -> 2% of each run, Pallas kernels for 0% -> 0%
where the time goes in v1:
time: 67.7 us; the launch traced here: 67.2 us
  Pallas kernels  44.8 us (66%)
  starting transfers between devices  8.11 us (12%)
  local copies, waits for them, and re-layouts  7.68 us (11%)
  waiting for transfers between devices  6.01 us (9%)
    pallas_call x1, Pallas kernels, per_device(): pl.pallas_call(functools.partial(reduce_kernel, n_row, n_col, owners, per...  37.7 us
    all_to_all x1, starting transfers between devices, per_device(): lax.all_to_all(jnp.broadcast_to(embedding[None], (n_col, *embedding.shape...  8.11 us
    pallas_call x1, Pallas kernels, per_device(): pl.pallas_call(functools.partial(compute_kernel, owners, per_owner, bins)...  7.1 us
    all_to_all x1, waiting for transfers between devices, per_device(): lax.all_to_all(jnp.broadcast_to(embedding[None], (n_col, *embedding.shape...  6.01 us
    unnamed x6, local copies, waits for them, and re-layouts  3.66 us
    broadcast_in_dim x1, local copies, waits for them, and re-layouts, per_device(): jnp.broadcast_to(embedding[None], (n_col, *embedding.shape))  1.47 us
  transfers between devices with their start and end apart: 1, of which 1 were waited for; matrix products, arithmetic and copies ran while one was open for 2% of the time, Pallas kernels for 0%

profile of v1, /device:TPU:1, one launch (start us, length us, event | category | flops | bytes accessed | tf_op | source)
XLA Modules:
  0.0 67.2 jit_solution(1037867371962814595)
XLA Ops:
  0.6 1.5 %broadcast_in_dim.12 = bf16[16,64,128]{2,1,0:T(8,128)(2,1)} broadcast(bf16[64,128]{1,0:T(8,128)(2,1)} %param.7), dimensions={1,2} | broadcast | bytes 278528 | tf_op jit(solution)/shard_map/broadcast_in_dim | solution.py:504
  2.1 0.0 copy-start
  2.1 8.1 %all-to-all-start = ((bf16[16,64,128]{2,1,0:T(8,128)(2,1)}), bf16[16,64,128]{2,1,0:T(8,128)(2,1)S(1)}, u32[]{:S(2)}, u32[]{:S(2)}) async-start(bf16[16,64,128]{2,1,0:T(8,128)(2,1)} %broadcast_in_dim.12), calls=%async_computation | async-start | bytes 524288 | tf_op jit(solution)/shard_map/all_to_all | solution.py:503
  10.2 0.0 copy-start.1
  10.2 0.6 copy-done.1
  10.9 0.7 %copy.10.mixb = f32[5,1]{1,0:T(8,128)} copy(f32[5,1]{0,1:T(1,128)S(1)} %bitcast.8) | data formatting | bytes 40 | tf_op jit(solution)/shard_map/broadcast_in_dim | solution.py:519
  11.6 0.0 copy-done
  11.6 0.6 pad.9.cot
  12.2 6.0 %all-to-all-done = bf16[16,64,128]{2,1,0:T(8,128)(2,1)S(1)} async-done(((bf16[16,64,128]{2,1,0:T(8,128)(2,1)}), bf16[16,64,128]{2,1,0:T(8,128)(2,1)S(1)}, u32[]{:S(2)}, u32[]{:S(2)}) %all-to-all-start) | async-done | bytes 262176 | tf_op jit(solution)/shard_map/all_to_all | solution.py:503
  18.2 0.6 pad_dynamic-slice_fusion.1.erow
  18.8 0.6 pad_dynamic-slice_fusion.ecol
  19.4 7.1 %shard_map.94 = (f32[5,32,64]{2,1,0:T(8,128)}, bf16[2,20,16,128]{3,2,1,0:T(8,128)(2,1)}) custom-call(s32[2]{0:T(128)} %dil.1, bf16[64,128]{1,0:T(8,128)(2,1)} %pad_dynamic-slice_fusion.1.erow, bf16[96,128]{1,0:T(8,128)(2,1)} %pad_dynamic-slice_fusion.ecol, bf16[3,3,48,128]{3,2,1,0:T(8,128)(2,1)} %kern.1, f32[1,48]{1,0:T(1,128)} %bitcast.7, ...), custom_call_target="tpu_custom_call" | custom-call | tf_op jit(solution)/shard_map/pallas_call | solution.py:510
  26.5 37.7 %shard_map.95 = (f32[64,128]{1,0:T(8,128)}, f32[27,16,128]{2,1,0:T(8,128)}) custom-call(bf16[2,20,16,128]{3,2,1,0:T(8,128)(2,1)} %get-tuple-element.8.send), custom_call_target="tpu_custom_call" | custom-call | tf_op jit(solution)/shard_map/pallas_call | solution.py:520
  64.2 1.4 %copy.13 = f32[64,128]{1,0:T(8,128)} copy(f32[64,128]{1,0:T(8,128)} %get-tuple-element.15) | data formatting | bytes 65536
  65.6 1.6 %copy.14 = f32[3,3,48,128]{3,2,1,0:T(8,128)} copy(f32[3,3,48,128]{3,2,1,0:T(8,128)} %bitcast.6) | data formatting | bytes 442368
Async XLA Ops:
  2.1 9.5 %copy-start = (bf16[5,32,64]{2,1,0:T(8,128)(2,1)S(1)}, bf16[5,32,64]{2,1,0:T(8,128)(2,1)}, u32[]{:S(2)}) copy-start(bf16[5,32,64]{2,1,0:T(8,128)(2,1)} %param.13) | copy-start | bytes 61444
  2.1 16.1 %all-to-all-start = ((bf16[16,64,128]{2,1,0:T(8,128)(2,1)}), bf16[16,64,128]{2,1,0:T(8,128)(2,1)S(1)}, u32[]{:S(2)}, u32[]{:S(2)}) async-start(bf16[16,64,128]{2,1,0:T(8,128)(2,1)} %broadcast_in_dim.12), calls=%async_computation | async-start | bytes 524288 | tf_op jit(solution)/shard_map/all_to_all | solution.py:503
  10.2 0.7 copy-start.1

commit v2 on v1

v2 whole, which is shorter than its diff:
```python
import functools

import jax
import jax.numpy as jnp
from jax import lax
from jax.experimental import pallas as pl
from jax.experimental.pallas import tpu as pltpu
from jax.sharding import PartitionSpec as P

MESH = pl.DeviceIdType.MESH
DMAX = 4
TILE = 16
LANES = 128
MIRROR = 64
GROUP = 8
TAPS = [(a, b) for a in range(3) for b in range(3)]
VM = pl.BlockSpec(memory_space=pltpu.VMEM)
SM = pl.BlockSpec(memory_space=pltpu.SMEM)


def f32(value):
    return value.astype(jnp.float32)


def b16(value):
    return value.astype(jnp.bfloat16)


def dot(a, b, dims):
    return lax.dot_general(a, b, (dims, ((), ())), preferred_element_type=jnp.float32)


def load_weights(kern, bias, mix, wconv, wall, bias_row, mix_rows):
    filters = kern.shape[2]
    wconv[...] = jnp.zeros_like(wconv)
    wall[...] = jnp.zeros_like(wall)
    bias_row[...] = jnp.zeros_like(bias_row)
    mix_rows[...] = jnp.zeros_like(mix_rows)
    for at in (0, MIRROR):
        bias_row[:, at : at + filters] = bias[...]
        mix_rows[0 : mix.shape[0], at : at + filters] = f32(mix[...])
    for n, (a, b) in enumerate(TAPS):
        tap = kern[a, b]
        wconv[0:filters, n * LANES : (n + 1) * LANES] = tap
        wconv[MIRROR : MIRROR + filters, (9 + n) * LANES : (10 + n) * LANES] = tap
        wall[b * LANES : b * LANES + filters, a * LANES : (a + 1) * LANES] = tap
        wall[a * LANES + MIRROR : a * LANES + MIRROR + filters, (3 + b) * LANES : (4 + b) * LANES] = tap


def shift_list(dil):
    return [-dil[0], 0, dil[0], -dil[1], 0, dil[1]]


def prepare(dil, place, cot, mr, mc, sm, cotf, mix_rows, guide, rows, cols, bins):
    row_rate, col_rate = dil[0], dil[1]
    lane_r = lax.broadcasted_iota(jnp.int32, (rows, LANES), 1)
    lane_c = lax.broadcasted_iota(jnp.int32, (cols, LANES), 1)
    row_at = lax.broadcasted_iota(jnp.int32, (rows, LANES), 0) + place.row * rows
    col_at = lax.broadcasted_iota(jnp.int32, (cols, LANES), 0) + place.col * cols

    def inside(at):
        return jnp.where((at >= 0) & (at < bins), 1.0, 0.0)

    for q, shift in enumerate(shift_list(dil)):
        mr[q] = inside(row_at + shift)
        mc[q] = b16(inside(col_at + shift))
    for n, t in enumerate((-1, 1)):
        mr[6 + n] = inside(row_at + jnp.where(lane_r < MIRROR, t * row_rate, t * col_rate))
        sm[n] = inside(col_at + jnp.where(lane_c < MIRROR, t * col_rate, t * row_rate))
    cotf[...] = f32(cot[...])
    mix16 = b16(mix_rows[...])
    for i in range(rows):
        guide[i * cols : (i + 1) * cols] = b16(0.5 * dot(b16(cotf[:, i, :]), mix16[0 : cotf.shape[0]], ((0,), (0,))))


def convolve(dil, erow, ecol, wconv, bias_row, er, ec, xr, xc, mr, mc, sm, lhs, guide, acts, sums, rows, cols):
    shifts = shift_list(dil)
    for k in range(erow.shape[0]):
        er[k * TILE : (k + 1) * TILE] = 0.5 * f32(erow[k])
    for k in range(ecol.shape[0]):
        ec[k * TILE : (k + 1) * TILE] = 0.5 * f32(ecol[k])
    for q, shift in enumerate(shifts):
        xr[q] = er[pl.ds(TILE + shift, rows), :]
        xc[q] = b16(ec[pl.ds(TILE + shift, cols), :])
    steps = cols // TILE
    group = GROUP
    last = cols - 8
    middle = jnp.zeros((cols, LANES), jnp.float32)
    border = [jnp.zeros((cols, LANES), jnp.float32) for _ in range(3)]
    for chunk in range(rows // group):
        buf = lhs.at[chunk % lhs.shape[0]]
        for ii in range(group):
            i = chunk * group + ii
            edge_row = i < DMAX or i >= rows - DMAX
            row16 = [b16(jnp.broadcast_to(xr[q, i : i + 1, :], (TILE, LANES))) for q in range(6)]
            if edge_row:
                rmask = [b16(jnp.broadcast_to(mr[q, i : i + 1, :], (TILE, LANES))) for q in range(6)]
            for n in range(18):
                a, b = TAPS[n % 9]
                p, q = (a, 3 + b) if n < 9 else (3 + b, a)
                for s in range(steps):
                    value = row16[p] + xc[q, s * TILE : (s + 1) * TILE, :]
                    if s in (0, steps - 1):
                        value = value * mc[q, s * TILE : (s + 1) * TILE, :]
                    if edge_row:
                        value = value * rmask[p]
                    at = ii * cols + s * TILE
                    buf[at : at + TILE, n * LANES : (n + 1) * LANES] = value
        conv = dot(buf[...], wconv[...], ((1,), (1,))) + bias_row[...]
        base = chunk * group * cols
        acts[base : base + group * cols] = b16(jnp.maximum(conv, 0.0))
        grad = jnp.where(conv > 0, f32(guide[base : base + group * cols]), 0.0)
        row_sums = [[], [], []]
        for ii in range(group):
            i = chunk * group + ii
            g = grad[ii * cols : (ii + 1) * cols]
            inner = g[8:16]
            for s in range(2, cols // 8 - 1):
                inner = inner + g[s * 8 : (s + 1) * 8]
            for t in range(3):
                first, final = g[0:8], g[last:cols]
                if t != 1:
                    first, final = first * sm[t // 2, 0:8], final * sm[t // 2, last:cols]
                row_sums[t].append(jnp.sum(inner + first + final, axis=0, keepdims=True))
            if i < DMAX or i >= rows - DMAX:
                for t in range(3):
                    mask = g if t == 1 else g * jnp.broadcast_to(mr[6 + t // 2, i : i + 1, :], g.shape)
                    border[t] = border[t] + mask
            else:
                middle = middle + g
        for t in range(3):
            for s in range(group // 8):
                sums[chunk * group + s * 8 : chunk * group + (s + 1) * 8, t * LANES : (t + 1) * LANES] = (
                    jnp.concatenate(row_sums[t][s * 8 : (s + 1) * 8], axis=0)
                )
    for t in range(3):
        sums[rows : rows + cols, t * LANES : (t + 1) * LANES] = pltpu.roll(middle + border[t], MIRROR, 1)


def kernel_part(sums, xr, xc, send, kernel_tiles):
    stacked = b16(sums[...])
    x = [jnp.concatenate([b16(xr[q]), xc[q]], axis=0) for q in range(6)]
    wide = dot(stacked, jnp.concatenate(x, axis=1), ((0,), (0,)))
    filters = 48
    pieces = []
    for a, b in TAPS:
        tap = (
            wide[b * LANES : b * LANES + filters, a * LANES : (a + 1) * LANES]
            + wide[a * LANES + MIRROR : a * LANES + MIRROR + filters, (3 + b) * LANES : (4 + b) * LANES]
        )
        pieces += [tap[s * TILE : (s + 1) * TILE] for s in range(filters // TILE)]
    zero = jnp.zeros((TILE, LANES), jnp.bfloat16)
    for k in range(2 * kernel_tiles):
        send[k % 2, k // 2] = b16(pieces[k]) if k < len(pieces) else zero


def embedding_part(dil, half, sums, wall, prow, pcol, send, kernel_tiles, rows, cols):
    shifts = shift_list(dil)
    emb = 0.5 * dot(b16(sums[...]), wall[...], ((1,), (0,)))
    for q in range(6):
        part = emb[:, q * LANES : (q + 1) * LANES]
        prow[q, 24 : 24 + rows] = part[0:rows]
        pcol[q, 24 : 24 + cols] = part[rows : rows + cols]
    row_grad = sum(prow[q, pl.ds(8 - shifts[q], rows + 2 * TILE), :] for q in range(6))
    col_grad = sum(pcol[q, pl.ds(8 - shifts[q], cols + 2 * TILE), :] for q in range(6))
    zero = jnp.zeros((TILE, LANES), jnp.bfloat16)
    for k in range(6):
        send[k // 3, kernel_tiles + k % 3] = b16(col_grad[k * TILE : (k + 1) * TILE])
        send[k // 3, kernel_tiles + 3 + k % 3] = zero
    for k in range(4):
        value = b16(row_grad[k * TILE : (k + 1) * TILE])

        @pl.when(half == 0)
        def _():
            send[k // 3, kernel_tiles + 3 + k % 3] = value

        @pl.when(half == 1)
        def _():
            send[(k + 2) // 3, kernel_tiles + 3 + (k + 2) % 3] = value


def mix_maps(acts, mix_rows, mixb, contact):
    maps, rows, cols = contact.shape
    mix16 = b16(mix_rows[...])
    step = 8
    for chunk in range(rows // step):
        act = acts[chunk * step * cols : (chunk + 1) * step * cols]
        mixed = 0.5 * dot(mix16, act, ((1,), (1,)))
        contact[:, chunk * step : (chunk + 1) * step, :] = jnp.stack(
            [mixed[0:maps, ii * cols : (ii + 1) * cols] + mixb[...] for ii in range(step)], axis=1
        )


def compute_scratch(rows, cols):
    return [
        pltpu.VMEM((LANES, 18 * LANES), jnp.bfloat16),
        pltpu.VMEM((3 * LANES, 6 * LANES), jnp.bfloat16),
        pltpu.VMEM((1, LANES), jnp.float32),
        pltpu.VMEM((8, LANES), jnp.float32),
        pltpu.VMEM((rows + 2 * TILE, LANES), jnp.float32),
        pltpu.VMEM((cols + 2 * TILE, LANES), jnp.float32),
        pltpu.VMEM((6, rows, LANES), jnp.float32),
        pltpu.VMEM((6, cols, LANES), jnp.bfloat16),
        pltpu.VMEM((8, rows, LANES), jnp.float32),
        pltpu.VMEM((6, cols, LANES), jnp.bfloat16),
        pltpu.VMEM((2, cols, LANES), jnp.float32),
        pltpu.VMEM((5, rows, cols), jnp.float32),
        pltpu.VMEM((2, GROUP * cols, 18 * LANES), jnp.bfloat16),
        pltpu.VMEM((rows * cols, LANES), jnp.bfloat16),
        pltpu.VMEM((rows * cols, LANES), jnp.bfloat16),
        pltpu.VMEM((rows + cols, 3 * LANES), jnp.float32),
        pltpu.VMEM((6, rows + 48, LANES), jnp.float32),
        pltpu.VMEM((6, cols + 48, LANES), jnp.float32),
    ]


class Place:
    def __init__(self, n_row, n_col):
        self.n_col = n_col
        self.n_z = n_row // 4
        self.row = lax.axis_index("row")
        self.col = lax.axis_index("col")
        self.half = lax.rem(self.row, 2)
        self.chip = self.row // 2
        self.z = lax.rem(self.chip, self.n_z)
        self.y = self.chip // self.n_z
        self.partner = self.row + 1 - 2 * self.half
        self.far = lax.rem(self.row + n_row // 2, n_row)

    def z_peer(self, z):
        return self.row + 2 * (z - self.z)

    def plane_row(self, y):
        return self.row + 2 * self.n_z * (y - self.y)

    def plane(self):
        return [(y, c) for y in range(2) for c in range(self.n_col)]

    def is_me(self, y, c):
        return (self.y == y) & (self.col == c)


def greet_all(place, barrier):
    n_col, n_z = place.n_col, place.n_z
    to = [(place.partner, place.col)]
    to += [(place.row, lax.rem(place.col + d, n_col)) for d in range(1, n_col)]
    to += [(place.z_peer(lax.rem(place.z + d, n_z)), place.col) for d in range(1, n_z)]
    to += [(place.far, lax.rem(place.col + d, n_col)) for d in range(n_col)]
    to += [(place.partner, lax.rem(place.col + d, n_col)) for d in (1, n_col - 1)]
    for device in to:
        pl.semaphore_signal(barrier, inc=1, device_id=device, device_id_type=MESH)
    return len(to)


def remote(src, dst, send_sem, recv_sem, row, col):
    return pltpu.make_async_remote_copy(
        src_ref=src, dst_ref=dst, send_sem=send_sem, recv_sem=recv_sem, device_id=(row, col), device_id_type=MESH
    )


def total(ref, count):
    value = f32(ref[0])
    for k in range(1, count):
        value = value + f32(ref[k])
    return value


class Exchange:
    def __init__(self, place, emb, erow, ecol, main_s, side_s, edge_s, recv_s):
        self.p, self.emb, self.erow, self.ecol = place, emb, erow, ecol
        self.main_s, self.side_s, self.edge_s, self.recv_s = main_s, side_s, edge_s, recv_s
        half = place.half
        self.side = place.chip - 1 + 2 * half
        self.side_ok = (self.side >= 0) & (self.side < place.n_col)
        self.low_ok = place.col > 0
        self.high_ok = place.col < place.n_col - 1

    def main(self, dst):
        h = self.p.half
        return remote(
            self.emb.at[pl.ds(h, 3)], self.erow.at[pl.ds(1 - h, 3)],
            self.main_s.at[dst], self.recv_s.at[0], self.p.row, dst,
        )

    def margin(self, dst):
        h = self.p.half
        return remote(
            self.emb.at[3 - 3 * h], self.erow.at[3 * h],
            self.side_s.at[dst], self.recv_s.at[1], self.p.row, dst,
        )

    def up(self, dst):
        return remote(self.emb.at[3], self.ecol.at[0], self.edge_s.at[0], self.recv_s.at[2], self.p.row, dst)

    def down(self, dst):
        return remote(self.emb.at[0], self.ecol.at[5], self.edge_s.at[1], self.recv_s.at[3], self.p.row, dst)

    def start(self):
        p = self.p
        for k, (owner, copy) in enumerate(((p.chip, self.main), (self.side, self.margin))):

            @pl.when(p.col == owner)
            def _():
                for dst in range(p.n_col):

                    @pl.when(p.col != dst)
                    def _():
                        copy(dst).start()

        @pl.when(self.high_ok)
        def _():
            self.up(p.col + 1).start()

        @pl.when(self.low_ok)
        def _():
            self.down(p.col - 1).start()

    def local(self):
        p = self.p
        for k in range(4):
            self.ecol[1 + k] = self.emb[k]

        @pl.when(p.col == p.chip)
        def _():
            for k in range(3):
                self.erow[1 - p.half + k] = self.emb[p.half + k]

        @pl.when(p.col == self.side)
        def _():
            self.erow[3 * p.half] = self.emb[3 - 3 * p.half]

        zero = jnp.zeros(self.emb.shape[1:], self.emb.dtype)

        @pl.when(jnp.logical_not(self.side_ok))
        def _():
            self.erow[3 * p.half] = zero

        @pl.when(jnp.logical_not(self.low_ok))
        def _():
            self.ecol[0] = zero

        @pl.when(jnp.logical_not(self.high_ok))
        def _():
            self.ecol[5] = zero

    def finish(self):
        p = self.p

        @pl.when(p.col != p.chip)
        def _():
            self.main(p.col).wait_recv()

        @pl.when((p.col != self.side) & self.side_ok)
        def _():
            self.margin(p.col).wait_recv()

        @pl.when(self.low_ok)
        def _():
            self.up(p.col).wait_recv()

        @pl.when(self.high_ok)
        def _():
            self.down(p.col).wait_recv()

    def sent(self):
        p = self.p
        for owner, copy in ((p.chip, self.main), (self.side, self.margin)):

            @pl.when(p.col == owner)
            def _():
                for dst in range(p.n_col):

                    @pl.when(p.col != dst)
                    def _():
                        copy(dst).wait_send()

        @pl.when(self.high_ok)
        def _():
            self.up(p.col).wait_send()

        @pl.when(self.low_ok)
        def _():
            self.down(p.col).wait_send()


def fused_kernel(
    n_row, n_col, owners, per_owner, rows, cols, bins,
    dil, emb, kern, bias, mix, mixb, cot,
    contact, kernel_out, emb_out,
    *scratch,
):
    place = Place(n_row, n_col)
    n_z = place.n_z
    row, col, half = place.row, place.col, place.half
    kt = per_owner * owners
    n_compute = 18
    (wconv, wall, bias_row, mix_rows, er, ec, xr, xc, mr, mc, sm, cotf, lhs, guide, acts, sums, prow, pcol) = scratch[
        :n_compute
    ]
    (
        erow, ecol, send, core_in, own, r_kernel, r_row, p_emb, y_emb, z_kernel, z_emb, full, emb_all, margins,
        main_s, side_s, edge_s, recv_s, core_s, kern_s, row_s, y_s, zk_s, ze_s, ag_s, agc_s, fin_s,
    ) = scratch[n_compute:]

    margins[...] = jnp.zeros_like(margins)
    barrier = pltpu.get_barrier_semaphore()
    count = greet_all(place, barrier)
    load_weights(kern, bias, mix, wconv, wall, bias_row, mix_rows)
    pl.semaphore_wait(barrier, count)

    exchange = Exchange(place, emb, erow, ecol, main_s, side_s, edge_s, recv_s)
    exchange.start()
    exchange.local()
    prow[...] = jnp.zeros_like(prow)
    pcol[...] = jnp.zeros_like(pcol)
    prepare(dil, place, cot, mr, mc, sm, cotf, mix_rows, guide, rows, cols, bins)
    exchange.finish()

    convolve(dil, erow, ecol, wconv, bias_row, er, ec, xr, xc, mr, mc, sm, lhs, guide, acts, sums, rows, cols)

    kernel_part(sums, xr, xc, send, kt)

    def swap(n, at, size):
        return remote(
            send.at[1 - half, pl.ds(at, size)], core_in.at[pl.ds(at, size)],
            core_s.at[0, n], core_s.at[1, n], place.partner, col,
        )

    swap(0, 0, kt).start()
    embedding_part(dil, half, sums, wall, prow, pcol, send, kt, rows, cols)
    swap(1, kt, 6).start()

    def owner_of(n):
        return place.plane_row(n % 2), n

    owner = (col < owners) & (lax.rem(col, 2) == place.y)

    def kernel_copy(slot, n):
        to_row, to_col = owner_of(n)
        return remote(
            own.at[pl.ds(n * per_owner, per_owner)], r_kernel.at[slot],
            kern_s.at[0, n], kern_s.at[1, slot], to_row, to_col,
        )

    my_slot = place.y * n_col + col
    swap(0, 0, kt).wait()
    own[0:kt] = b16(f32(send[half, 0:kt]) + f32(core_in[0:kt]))
    for n in range(owners):

        @pl.when(jnp.logical_not(place.is_me(n % 2, n)))
        def _():
            kernel_copy(my_slot, n).start()

    def row_copy(src):
        return remote(own.at[pl.ds(kt + 3, 3)], r_row.at[src], row_s.at[n_col], row_s.at[src], row, place.chip)

    swap(1, kt, 6).wait()
    own[kt : kt + 6] = b16(f32(send[half, kt : kt + 6]) + f32(core_in[kt : kt + 6]))

    @pl.when(col != place.chip)
    def _():
        row_copy(col).start()

    @pl.when(owner)
    def _():
        r_kernel[my_slot] = own[pl.ds(col * per_owner, per_owner)]

    @pl.when(col == place.chip)
    def _():
        r_row[col] = own[kt + 3 : kt + 6]

    mix_maps(acts, mix_rows, mixb, contact)

    far_copy = remote(p_emb, y_emb, y_s.at[0], y_s.at[1], place.far, col)

    def z_copy(sems, buf, src, dst):
        return remote(buf.at[src], buf.at[src], sems.at[0, dst], sems.at[1, src], place.z_peer(dst), col)

    def kernel_in(slot):
        return remote(
            own.at[pl.ds(0, per_owner)], r_kernel.at[slot], kern_s.at[0, 0], kern_s.at[1, slot], row, col
        )

    @pl.when(owner)
    def _():
        for slot, (y, c) in enumerate(place.plane()):

            @pl.when(jnp.logical_not(place.is_me(y, c)))
            def _():
                kernel_in(slot).wait_recv()

        z_kernel[place.z] = b16(total(r_kernel, 2 * n_col))
        for dst in range(n_z):

            @pl.when(dst != place.z)
            def _():
                z_copy(zk_s, z_kernel, place.z, dst).start()

    mine = f32(own[kt : kt + 3])

    @pl.when(col != place.chip)
    def _():
        p_emb[...] = b16(mine)

    @pl.when(col == place.chip)
    def _():
        for src in range(n_col):

            @pl.when(src != col)
            def _():
                row_copy(src).wait_recv()

        p_emb[...] = b16(mine + total(r_row, n_col))

    far_copy.start()

    def gather_copy(n, y, c):
        return remote(full.at[half, n], full.at[half, n], ag_s.at[0, y * n_col + c], ag_s.at[1, n], place.plane_row(y), c)

    @pl.when(owner)
    def _():
        for src in range(n_z):

            @pl.when(src != place.z)
            def _():
                z_copy(zk_s, z_kernel, src, place.z).wait_recv()

        full[half, col] = b16(total(z_kernel, n_z))
        for y, c in place.plane():

            @pl.when(jnp.logical_not(place.is_me(y, c)))
            def _():
                gather_copy(col, y, c).start()

    far_copy.wait()
    z_emb[place.z] = b16(f32(p_emb[...]) + f32(y_emb[...]))
    for dst in range(n_z):

        @pl.when(dst != place.z)
        def _():
            z_copy(ze_s, z_emb, place.z, dst).start()

    for src in range(n_z):

        @pl.when(src != place.z)
        def _():
            z_copy(ze_s, z_emb, src, place.z).wait_recv()

    emb_all[half] = b16(total(z_emb, n_z))
    emb_swap = remote(emb_all.at[half], emb_all.at[half], fin_s.at[0, 0], fin_s.at[1, 0], place.partner, col)
    emb_swap.start()
    to = col - 1 + 2 * half
    exists = (to >= 0) & (to < n_col)
    came = col + 1 - 2 * half
    came_ok = (came >= 0) & (came < n_col)

    def margin_copy(n, slot, device_row, device_col):
        return remote(
            emb_all.at[half, 2 * half], margins.at[slot],
            fin_s.at[0, 1 + n], fin_s.at[1, 1 + n], device_row, device_col,
        )

    @pl.when(exists)
    def _():
        margin_copy(0, half, row, to).start()
        margin_copy(1, half, place.partner, to).start()

    for n in range(owners):

        @pl.when(jnp.logical_not(place.is_me(n % 2, n)))
        def _():
            gather_copy(n, place.y, col).wait_recv()

    share = remote(full.at[half], full.at[half], agc_s.at[0], agc_s.at[1], place.partner, col)
    share.start()

    emb_swap.wait()

    @pl.when(came_ok)
    def _():
        margin_copy(0, half, row, col).wait_recv()

    @pl.when(exists)
    def _():
        margin_copy(1, 1 - half, row, col).wait_recv()

    main = [f32(emb_all[0, 1]), f32(emb_all[0, 2]), f32(emb_all[1, 0]), f32(emb_all[1, 1])]
    emb_out[0] = main[0] + f32(margins[1])
    emb_out[1] = main[1]
    emb_out[2] = main[2]
    emb_out[3] = main[3] + f32(margins[0])

    exchange.sent()
    for n in range(owners):

        @pl.when(jnp.logical_not(place.is_me(n % 2, n)))
        def _():
            kernel_copy(my_slot, n).wait_send()

    @pl.when(col != place.chip)
    def _():
        row_copy(col).wait_send()

    for dst in range(n_z):

        @pl.when((dst != place.z) & owner)
        def _():
            z_copy(zk_s, z_kernel, place.z, dst).wait_send()

        @pl.when(dst != place.z)
        def _():
            z_copy(ze_s, z_emb, place.z, dst).wait_send()

    @pl.when(owner)
    def _():
        for y, c in place.plane():

            @pl.when(jnp.logical_not(place.is_me(y, c)))
            def _():
                gather_copy(col, y, c).wait_send()

    @pl.when(exists)
    def _():
        margin_copy(0, half, row, to).wait_send()
        margin_copy(1, half, place.partner, to).wait_send()

    share.wait()
    kernel_out[...] = full[...]


def fused_scratch(n_row, n_col, owners, per_owner):
    n_z = n_row // 4
    kt = owners * per_owner

    def tiles(*lead):
        return pltpu.VMEM((*lead, TILE, LANES), jnp.bfloat16)

    def sems(*shape):
        return pltpu.SemaphoreType.DMA(shape)

    return [
        tiles(4), tiles(6), tiles(2, kt + 6), tiles(kt + 6), tiles(kt + 6), tiles(2 * n_col, per_owner), tiles(n_col, 3),
        tiles(3), tiles(3), tiles(n_z, per_owner), tiles(n_z, 3), tiles(2, owners, per_owner), tiles(2, 3), tiles(2),
        sems(n_col), sems(n_col), sems(2), sems(4), sems(2, 2), sems(2, 2 * n_col), sems(n_col + 1), sems(2),
        sems(2, n_z), sems(2, n_z), sems(2, 2 * n_col), sems(2), sems(2, 3),
    ]


def finish_kernel(per_owner, contact, grad, emb, contact_out, grad_out, emb_out):
    contact_out[...] = contact[...]
    emb_out[...] = emb[...]
    for k in range(grad_out.shape[0]):
        grad_out[k] = f32(grad[k % 2, k // (2 * per_owner), (k // 2) % per_owner])


def per_device(n_row, n_col, embedding, dilation, kernel, kernel_bias, mixing, mixing_bias, cotangent):
    channels = embedding.shape[1]
    filters = kernel.shape[2]
    maps, rows, cols = cotangent.shape
    bins = cols * n_col
    count = 9 * filters // TILE
    per_owner = -(-count // (2 * n_col))
    owners = -(-count // (2 * per_owner))
    contact, grad, emb = pl.pallas_call(
        functools.partial(fused_kernel, n_row, n_col, owners, per_owner, rows, cols, bins),
        out_shape=[
            jax.ShapeDtypeStruct((maps, rows, cols), jnp.float32),
            jax.ShapeDtypeStruct((2, owners, per_owner, TILE, channels), jnp.bfloat16),
            jax.ShapeDtypeStruct((cols // TILE, TILE, channels), jnp.float32),
        ],
        in_specs=[SM, VM, VM, VM, VM, VM, VM],
        out_specs=[VM, VM, VM],
        scratch_shapes=compute_scratch(rows, cols) + fused_scratch(n_row, n_col, owners, per_owner),
        compiler_params=pltpu.CompilerParams(collective_id=0, has_side_effects=True),
    )(
        dilation,
        embedding.reshape(cols // TILE, TILE, channels),
        kernel,
        kernel_bias[None],
        mixing,
        mixing_bias[:, None],
        cotangent,
    )
    contact, grad, emb = pl.pallas_call(
        functools.partial(finish_kernel, per_owner),
        out_shape=[
            jax.ShapeDtypeStruct((maps, rows, cols), jnp.float32),
            jax.ShapeDtypeStruct((count, TILE, channels), jnp.float32),
            jax.ShapeDtypeStruct((cols // TILE, TILE, channels), jnp.float32),
        ],
        in_specs=[VM, VM, VM],
        out_specs=[VM, VM, VM],
    )(contact, grad, emb)
    return contact, emb.reshape(cols, channels), grad.reshape(3, 3, filters, channels)


def solution(mesh):
    return jax.shard_map(
        functools.partial(per_device, mesh.shape["row"], mesh.shape["col"]),
        mesh=mesh,
        in_specs=(P("col", None), P(), P(), P(), P(), P(), P(None, "row", "col")),
        out_specs=(P(None, "row", "col"), P("col", None), P()),
        check_vma=False,
    )
```

time: 67.7 us -> 52.8 us (0.78)
  starting transfers between devices: 8.11 us -> 0 us
  local copies, waits for them, and re-layouts: 7.68 us -> 1.33 us
  waiting for transfers between devices: 6.01 us -> 0 us
  Pallas kernels: 44.8 us -> 50.6 us
    all_to_all x1 -> x0, starting transfers between devices: 8.11 us -> none  [per_device(): lax.all_to_all(jnp.broadcast_to(embedding[None], (n_col, *embedding.shape...]
    all_to_all x1 -> x0, waiting for transfers between devices: 6.01 us -> none  [per_device(): lax.all_to_all(jnp.broadcast_to(embedding[None], (n_col, *embedding.shape...]
    pallas_call x2, Pallas kernels: 44.8 us -> 50.6 us  [the longest x1 48.9 us: per_device(): pl.pallas_call(functools.partial(fused_kernel, n_row, n_col, owners, per_...]
    unnamed x6 -> x2, local copies, waits for them, and re-layouts: 3.66 us -> 0.65 us
    broadcast_in_dim x1 -> x0, local copies, waits for them, and re-layouts: 1.47 us -> none  [per_device(): jnp.broadcast_to(embedding[None], (n_col, *embedding.shape))]
    dynamic_slice x2 -> x0, local copies, waits for them, and re-layouts: 1.23 us -> none  [the longest x1 0.62 us: per_device(): ecol = lax.dynamic_slice_in_dim(padded, col_start, cols + 2 * TILE, 0)]
  transfers between devices with their start and end apart: 1 -> 0, of which waited for: 1 -> 0; matrix products, arithmetic and copies ran while one was open for 2% -> 0% of each run, Pallas kernels for 0% -> 0%
where the time goes in v2:
time: 52.8 us; the launch traced here: 52.6 us
  Pallas kernels  50.6 us (96%)
  local copies, waits for them, and re-layouts  1.33 us (3%)
  between operations  0.65 us (1%)
    pallas_call x1, Pallas kernels, per_device(): pl.pallas_call(functools.partial(fused_kernel, n_row, n_col, owners, per_...  48.9 us
    pallas_call x1, Pallas kernels, per_device(): pl.pallas_call(functools.partial(finish_kernel, per_owner), out_shape=[ja...  1.68 us

profile of v2, /device:TPU:1, one launch (start us, length us, event | category | flops | bytes accessed | tf_op | source)
XLA Modules:
  0.0 52.6 jit_solution(6267160505100742659)
XLA Ops:
  0.6 0.0 copy-start
  0.6 0.6 %copy-done = f32[5]{0:T(128)S(1)} copy-done((f32[5]{0:T(128)S(1)}, f32[5]{0:T(128)}, u32[]{:S(2)}) %copy-start) | copy-done | bytes 44
  1.3 0.7 %copy.10.mixb = f32[5,1]{1,0:T(8,128)} copy(f32[5,1]{0,1:T(1,128)S(1)} %bitcast.7) | data formatting | bytes 40 | tf_op jit(solution)/shard_map/broadcast_in_dim | solution.py:681
  2.0 48.9 %shard_map.94 = (f32[5,32,64]{2,1,0:T(8,128)}, bf16[2,14,1,16,128]{4,3,2,1,0:T(8,128)(2,1)}, f32[4,16,128]{2,1,0:T(8,128)}) custom-call(s32[2]{0:T(128)} %dil.1, bf16[4,16,128]{2,1,0:T(8,128)(2,1)} %bitcast.5, bf16[3,3,48,128]{3,2,1,0:T(8,128)(2,1)} %kern.1, f32[1,48]{1,0:T(1,128)} %bitcast.6, bf16[5,48]{1,0:T(8,128)(2,1)} %mix.1, f32[5,1]{1,0:T(8,128)} %copy.10.mixb, ...), custom_call_target="tpu_custom_call" | custom-call | tf_op jit(solution)/shard_map/pallas_call | solution.py:664
  50.9 1.7 %shard_map.95 = (f32[5,32,64]{2,1,0:T(8,128)}, f32[27,16,128]{2,1,0:T(8,128)}, f32[4,16,128]{2,1,0:T(8,128)}) custom-call(f32[5,32,64]{2,1,0:T(8,128)} %get-tuple-element.9.contact, bf16[2,14,1,16,128]{4,3,2,1,0:T(8,128)(2,1)} %get-tuple-element.10.grad, f32[4,16,128]{2,1,0:T(8,128)} %get-tuple-element.11.emb), custom_call_target="tpu_custom_call" | custom-call | tf_op jit(solution)/shard_map/pallas_call | solution.py:684
Async XLA Ops:
  0.6 0.7 %copy-start = (f32[5]{0:T(128)S(1)}, f32[5]{0:T(128)}, u32[]{:S(2)}) copy-start(f32[5]{0:T(128)} %param.12) | copy-start | bytes 64

commit v3 on v2

--- a/solution.py
+++ b/solution.py
@@ -13,6 +13,9 @@
 LANES = 128
 MIRROR = 64
 GROUP = 8
+N_LO = 4
+VMEM = 20 << 20
+NEAR = (-1, 0, 1, 2)
 TAPS = [(a, b) for a in range(3) for b in range(3)]
 VM = pl.BlockSpec(memory_space=pltpu.VMEM)
 SM = pl.BlockSpec(memory_space=pltpu.SMEM)
@@ -183,11 +186,15 @@
     maps, rows, cols = contact.shape
     mix16 = b16(mix_rows[...])
     step = 8
+    at = lax.broadcasted_iota(jnp.int32, (8, step * cols), 0)
+    offset = jnp.zeros((8, step * cols), jnp.float32)
+    for t in range(maps):
+        offset = jnp.where(at == t, mixb[t], offset)
     for chunk in range(rows // step):
         act = acts[chunk * step * cols : (chunk + 1) * step * cols]
-        mixed = 0.5 * dot(mix16, act, ((1,), (1,)))
+        mixed = 0.5 * dot(mix16, act, ((1,), (1,))) + offset
         contact[:, chunk * step : (chunk + 1) * step, :] = jnp.stack(
-            [mixed[0:maps, ii * cols : (ii + 1) * cols] + mixb[...] for ii in range(step)], axis=1
+            [mixed[0:maps, ii * cols : (ii + 1) * cols] for ii in range(step)], axis=1
         )
 
 
@@ -224,6 +231,11 @@
         self.chip = self.row // 2
         self.z = lax.rem(self.chip, self.n_z)
         self.y = self.chip // self.n_z
+        self.n_lo = N_LO
+        self.n_x = n_col // N_LO
+        self.n_y = 2 * N_LO
+        self.x = self.col // N_LO
+        self.yy = self.y * N_LO + lax.rem(self.col, N_LO)
         self.partner = self.row + 1 - 2 * self.half
         self.far = lax.rem(self.row + n_row // 2, n_row)
 
@@ -232,6 +244,12 @@
 
     def plane_row(self, y):
         return self.row + 2 * self.n_z * (y - self.y)
+
+    def turn(self, step):
+        return lax.rem(self.yy + step + self.n_y, self.n_y)
+
+    def at(self, x, yy):
+        return self.plane_row(yy // self.n_lo), x * self.n_lo + lax.rem(yy, self.n_lo)
 
     def plane(self):
         return [(y, c) for y in range(2) for c in range(self.n_col)]
@@ -243,13 +261,22 @@
 def greet_all(place, barrier):
     n_col, n_z = place.n_col, place.n_z
     to = [(place.partner, place.col)]
-    to += [(place.row, lax.rem(place.col + d, n_col)) for d in range(1, n_col)]
+    to += [
+        place.at(lax.rem(place.x + dx, place.n_x), place.turn(dy))
+        for dx in range(place.n_x)
+        for dy in (-2, -1, 0, 1, 2)
+        if dx or dy
+    ]
     to += [(place.z_peer(lax.rem(place.z + d, n_z)), place.col) for d in range(1, n_z)]
-    to += [(place.far, lax.rem(place.col + d, n_col)) for d in range(n_col)]
     to += [(place.partner, lax.rem(place.col + d, n_col)) for d in (1, n_col - 1)]
     for device in to:
         pl.semaphore_signal(barrier, inc=1, device_id=device, device_id_type=MESH)
     return len(to)
+
+
+def greet_far(place, second):
+    for dy in (-2, 2):
+        pl.semaphore_signal(second, inc=1, device_id=place.at(place.x, place.turn(dy)), device_id_type=MESH)
 
 
 def remote(src, dst, send_sem, recv_sem, row, col):
@@ -269,51 +296,78 @@
     def __init__(self, place, emb, erow, ecol, main_s, side_s, edge_s, recv_s):
         self.p, self.emb, self.erow, self.ecol = place, emb, erow, ecol
         self.main_s, self.side_s, self.edge_s, self.recv_s = main_s, side_s, edge_s, recv_s
-        half = place.half
+        half, col, z = place.half, place.col, place.z
         self.side = place.chip - 1 + 2 * half
         self.side_ok = (self.side >= 0) & (self.side < place.n_col)
-        self.low_ok = place.col > 0
-        self.high_ok = place.col < place.n_col - 1
-
-    def main(self, dst):
+        self.low_ok = col > 0
+        self.high_ok = col < place.n_col - 1
+        self.main_src = (col == z) | (col == place.n_z + z)
+        self.main_y = jnp.where(col == z, 0, 1)
+        side = z - 1 + 2 * half
+        self.side_src = (col == side) | (col == place.n_z + side)
+        self.side_y = jnp.where(col == side, 0, 1)
+
+    def targets(self, for_y):
+        p = self.p
+        for k, dy in enumerate(NEAR):
+            yy = p.turn(dy)
+            for x in range(p.n_x):
+                wanted = yy // p.n_lo == for_y
+                if dy == 0:
+                    wanted = wanted & (x != p.x)
+                yield k * p.n_x + x, wanted, *p.at(x, yy)
+
+    def main(self, slot, row, col):
         h = self.p.half
         return remote(
             self.emb.at[pl.ds(h, 3)], self.erow.at[pl.ds(1 - h, 3)],
-            self.main_s.at[dst], self.recv_s.at[0], self.p.row, dst,
-        )
-
-    def margin(self, dst):
+            self.main_s.at[slot], self.recv_s.at[0], row, col,
+        )
+
+    def margin(self, slot, row, col):
         h = self.p.half
         return remote(
             self.emb.at[3 - 3 * h], self.erow.at[3 * h],
-            self.side_s.at[dst], self.recv_s.at[1], self.p.row, dst,
-        )
-
-    def up(self, dst):
-        return remote(self.emb.at[3], self.ecol.at[0], self.edge_s.at[0], self.recv_s.at[2], self.p.row, dst)
-
-    def down(self, dst):
-        return remote(self.emb.at[0], self.ecol.at[5], self.edge_s.at[1], self.recv_s.at[3], self.p.row, dst)
+            self.side_s.at[slot], self.recv_s.at[1], row, col,
+        )
+
+    def up(self):
+        p = self.p
+        row = p.plane_row(p.turn(1) // p.n_lo)
+        return remote(self.emb.at[3], self.ecol.at[0], self.edge_s.at[0], self.recv_s.at[2], row, p.col + 1)
+
+    def down(self):
+        p = self.p
+        row = p.plane_row(p.turn(-1) // p.n_lo)
+        return remote(self.emb.at[0], self.ecol.at[5], self.edge_s.at[1], self.recv_s.at[3], row, p.col - 1)
+
+    def outgoing(self, act):
+        for source, for_y, copy in (
+            (self.main_src, self.main_y, self.main),
+            (self.side_src, self.side_y, self.margin),
+        ):
+
+            @pl.when(source)
+            def _():
+                for slot, wanted, row, col in self.targets(for_y):
+
+                    @pl.when(wanted)
+                    def _():
+                        act(copy(slot, row, col))
+
+        @pl.when(self.high_ok)
+        def _():
+            act(self.up())
+
+        @pl.when(self.low_ok)
+        def _():
+            act(self.down())
 
     def start(self):
-        p = self.p
-        for k, (owner, copy) in enumerate(((p.chip, self.main), (self.side, self.margin))):
-
-            @pl.when(p.col == owner)
-            def _():
-                for dst in range(p.n_col):
-
-                    @pl.when(p.col != dst)
-                    def _():
-                        copy(dst).start()
-
-        @pl.when(self.high_ok)
-        def _():
-            self.up(p.col + 1).start()
-
-        @pl.when(self.low_ok)
-        def _():
-            self.down(p.col - 1).start()
+        self.outgoing(lambda copy: copy.start())
+
+    def sent(self):
+        self.outgoing(lambda copy: copy.wait_send())
 
     def local(self):
         p = self.p
@@ -348,44 +402,24 @@
 
         @pl.when(p.col != p.chip)
         def _():
-            self.main(p.col).wait_recv()
+            self.main(0, p.row, p.col).wait_recv()
 
         @pl.when((p.col != self.side) & self.side_ok)
         def _():
-            self.margin(p.col).wait_recv()
+            self.margin(0, p.row, p.col).wait_recv()
 
         @pl.when(self.low_ok)
         def _():
-            self.up(p.col).wait_recv()
+            self.up().wait_recv()
 
         @pl.when(self.high_ok)
         def _():
-            self.down(p.col).wait_recv()
-
-    def sent(self):
-        p = self.p
-        for owner, copy in ((p.chip, self.main), (self.side, self.margin)):
-
-            @pl.when(p.col == owner)
-            def _():
-                for dst in range(p.n_col):
-
-                    @pl.when(p.col != dst)
-                    def _():
-                        copy(dst).wait_send()
-
-        @pl.when(self.high_ok)
-        def _():
-            self.up(p.col).wait_send()
-
-        @pl.when(self.low_ok)
-        def _():
-            self.down(p.col).wait_send()
+            self.down().wait_recv()
 
 
 def fused_kernel(
     n_row, n_col, owners, per_owner, rows, cols, bins,
-    dil, emb, kern, bias, mix, mixb, cot,
+    dil_h, emb_h, kern_h, bias_h, mix_h, mixb_h, cot_h,
     contact, kernel_out, emb_out,
     *scratch,
 ):
@@ -400,19 +434,32 @@
     (
         erow, ecol, send, core_in, own, r_kernel, r_row, p_emb, y_emb, z_kernel, z_emb, full, emb_all, margins,
         main_s, side_s, edge_s, recv_s, core_s, kern_s, row_s, y_s, zk_s, ze_s, ag_s, agc_s, fin_s,
+        second, emb, dil, kern, bias, mix, mixb, cot, load_s,
     ) = scratch[n_compute:]
 
     margins[...] = jnp.zeros_like(margins)
+    r_row[...] = jnp.zeros_like(r_row)
     barrier = pltpu.get_barrier_semaphore()
     count = greet_all(place, barrier)
-    load_weights(kern, bias, mix, wconv, wall, bias_row, mix_rows)
-    pl.semaphore_wait(barrier, count)
-
-    exchange = Exchange(place, emb, erow, ecol, main_s, side_s, edge_s, recv_s)
-    exchange.start()
-    exchange.local()
+    loads = [
+        pltpu.make_async_copy(src, dst, load_s.at[n])
+        for n, (src, dst) in enumerate(
+            ((emb_h, emb), (dil_h, dil), (kern_h, kern), (bias_h, bias), (mix_h, mix), (mixb_h, mixb), (cot_h, cot))
+        )
+    ]
+    for load in loads:
+        load.start()
     prow[...] = jnp.zeros_like(prow)
     pcol[...] = jnp.zeros_like(pcol)
+    for load in loads:
+        load.wait()
+    load_weights(kern, bias, mix, wconv, wall, bias_row, mix_rows)
+    exchange = Exchange(place, emb, erow, ecol, main_s, side_s, edge_s, recv_s)
+    exchange.local()
+    pl.semaphore_wait(barrier, count)
+
+    exchange.start()
+    greet_far(place, second)
     prepare(dil, place, cot, mr, mc, sm, cotf, mix_rows, guide, rows, cols, bins)
     exchange.finish()
 
@@ -443,6 +490,7 @@
         )
 
     my_slot = place.y * n_col + col
+    pl.semaphore_wait(second, 2)
     swap(0, 0, kt).wait()
     own[0:kt] = b16(f32(send[half, 0:kt]) + f32(core_in[0:kt]))
     for n in range(owners):
@@ -451,15 +499,19 @@
         def _():
             kernel_copy(my_slot, n).start()
 
-    def row_copy(src):
-        return remote(own.at[pl.ds(kt + 3, 3)], r_row.at[src], row_s.at[n_col], row_s.at[src], row, place.chip)
+    ahead = lax.rem(place.yy - lax.rem(place.chip, N_LO) + 1 + place.n_y, place.n_y)
+    row_slot = lax.rem(ahead, 4) * place.n_x + place.x
+    row_to = place.plane_row(jnp.where(ahead < 4, 0, 1))
+
+    def row_copy(slot):
+        return remote(own.at[pl.ds(kt + 3, 3)], r_row.at[slot], row_s.at[0], row_s.at[1 + slot], row_to, place.chip)
 
     swap(1, kt, 6).wait()
     own[kt : kt + 6] = b16(f32(send[half, kt : kt + 6]) + f32(core_in[kt : kt + 6]))
 
     @pl.when(col != place.chip)
     def _():
-        row_copy(col).start()
+        row_copy(row_slot).start()
 
     @pl.when(owner)
     def _():
@@ -467,7 +519,7 @@
 
     @pl.when(col == place.chip)
     def _():
-        r_row[col] = own[kt + 3 : kt + 6]
+        r_row[place.n_x + place.x] = own[kt + 3 : kt + 6]
 
     mix_maps(acts, mix_rows, mixb, contact)
 
@@ -498,19 +550,19 @@
 
     mine = f32(own[kt : kt + 3])
 
-    @pl.when(col != place.chip)
+    @pl.when(jnp.logical_not(exchange.main_src))
     def _():
         p_emb[...] = b16(mine)
 
-    @pl.when(col == place.chip)
-    def _():
-        for src in range(n_col):
-
-            @pl.when(src != col)
+    @pl.when(exchange.main_src)
+    def _():
+        for slot, wanted, _, _ in exchange.targets(exchange.main_y):
+
+            @pl.when(wanted)
             def _():
-                row_copy(src).wait_recv()
-
-        p_emb[...] = b16(mine + total(r_row, n_col))
+                row_copy(slot).wait_recv()
+
+        p_emb[...] = b16(mine + total(r_row, len(NEAR) * place.n_x))
 
     far_copy.start()
 
@@ -599,7 +651,7 @@
 
     @pl.when(col != place.chip)
     def _():
-        row_copy(col).wait_send()
+        row_copy(row_slot).wait_send()
 
     for dst in range(n_z):
 
@@ -628,7 +680,7 @@
     kernel_out[...] = full[...]
 
 
-def fused_scratch(n_row, n_col, owners, per_owner):
+def fused_scratch(n_row, n_col, owners, per_owner, loaded):
     n_z = n_row // 4
     kt = owners * per_owner
 
@@ -639,10 +691,11 @@
         return pltpu.SemaphoreType.DMA(shape)
 
     return [
-        tiles(4), tiles(6), tiles(2, kt + 6), tiles(kt + 6), tiles(kt + 6), tiles(2 * n_col, per_owner), tiles(n_col, 3),
+        tiles(4), tiles(6), tiles(2, kt + 6), tiles(kt + 6), tiles(kt + 6), tiles(2 * n_col, per_owner), tiles(4 * n_col // N_LO, 3),
         tiles(3), tiles(3), tiles(n_z, per_owner), tiles(n_z, 3), tiles(2, owners, per_owner), tiles(2, 3), tiles(2),
-        sems(n_col), sems(n_col), sems(2), sems(4), sems(2, 2), sems(2, 2 * n_col), sems(n_col + 1), sems(2),
+        sems(4 * n_col // N_LO), sems(4 * n_col // N_LO), sems(2), sems(4), sems(2, 2), sems(2, 2 * n_col), sems(1 + 4 * n_col // N_LO), sems(2),
         sems(2, n_z), sems(2, n_z), sems(2, 2 * n_col), sems(2), sems(2, 3),
+        pltpu.SemaphoreType.REGULAR, *loaded, sems(len(loaded)),
     ]
 
 
@@ -661,6 +714,15 @@
     count = 9 * filters // TILE
     per_owner = -(-count // (2 * n_col))
     owners = -(-count // (2 * per_owner))
+    loaded = [
+        pltpu.VMEM((cols // TILE, TILE, channels), jnp.bfloat16),
+        pltpu.SMEM((2,), jnp.int32),
+        pltpu.VMEM(kernel.shape, jnp.bfloat16),
+        pltpu.VMEM((1, filters), jnp.float32),
+        pltpu.VMEM(mixing.shape, jnp.bfloat16),
+        pltpu.SMEM((maps,), jnp.float32),
+        pltpu.VMEM(cotangent.shape, jnp.bfloat16),
+    ]
     contact, grad, emb = pl.pallas_call(
         functools.partial(fused_kernel, n_row, n_col, owners, per_owner, rows, cols, bins),
         out_shape=[
@@ -668,18 +730,23 @@
             jax.ShapeDtypeStruct((2, owners, per_owner, TILE, channels), jnp.bfloat16),
             jax.ShapeDtypeStruct((cols // TILE, TILE, channels), jnp.float32),
         ],
-        in_specs=[SM, VM, VM, VM, VM, VM, VM],
+        in_specs=[pl.BlockSpec(memory_space=pltpu.HBM)] * 7,
         out_specs=[VM, VM, VM],
-        scratch_shapes=compute_scratch(rows, cols) + fused_scratch(n_row, n_col, owners, per_owner),
-        compiler_params=pltpu.CompilerParams(collective_id=0, has_side_effects=True),
+        scratch_shapes=compute_scratch(rows, cols) + fused_scratch(n_row, n_col, owners, per_owner, loaded),
+        compiler_params=pltpu.CompilerParams(collective_id=0, has_side_effects=True, vmem_limit_bytes=VMEM),
     )(
-        dilation,
-        embedding.reshape(cols // TILE, TILE, channels),
-        kernel,
-        kernel_bias[None],
-        mixing,
-        mixing_bias[:, None],
-        cotangent,
+        *(
+            pltpu.with_memory_space_constraint(value, pltpu.HBM)
+            for value in (
+                dilation,
+                embedding.reshape(cols // TILE, TILE, channels),
+                kernel,
+                kernel_bias[None],
+                mixing,
+                mixing_bias,
+                cotangent,
+            )
+        )
     )
     contact, grad, emb = pl.pallas_call(
         functools.partial(finish_kernel, per_owner),
@@ -690,6 +757,7 @@
         ],
         in_specs=[VM, VM, VM],
         out_specs=[VM, VM, VM],
+        compiler_params=pltpu.CompilerParams(vmem_limit_bytes=VMEM),
     )(contact, grad, emb)
     return contact, emb.reshape(cols, channels), grad.reshape(3, 3, filters, channels)
 

time: 52.8 us -> 47.9 us (0.907)
  Pallas kernels: 50.6 us -> 47.1 us
  local copies, waits for them, and re-layouts: 1.33 us -> 0 us
    pallas_call x1, Pallas kernels: 48.9 us -> 46.3 us  [per_device(): pl.pallas_call(functools.partial(fused_kernel, n_row, n_col, owners, per_...]
    pallas_call x1, Pallas kernels: 1.68 us -> 0.74 us  [per_device(): pl.pallas_call(functools.partial(finish_kernel, per_owner), out_shape=[ja...]
    broadcast_in_dim x1 -> x0, local copies, waits for them, and re-layouts: 0.68 us -> none  [per_device(): mixing_bias[:, None]]
    unnamed x2 -> x0, local copies, waits for them, and re-layouts: 0.65 us -> none
where the time goes in v3:
time: 47.9 us; the launch traced here: 47.7 us
  Pallas kernels  47.1 us (98%)
  between operations  0.64 us (1%)
    pallas_call x1, Pallas kernels, per_device(): pl.pallas_call(functools.partial(fused_kernel, n_row, n_col, owners, per_...  46.3 us

profile of v3, /device:TPU:1, one launch (start us, length us, event | category | flops | bytes accessed | tf_op | source)
XLA Modules:
  0.0 47.7 jit_solution(11357693351166427581)
XLA Ops:
  0.6 46.3 %shard_map.94 = (f32[5,32,64]{2,1,0:T(8,128)S(1)}, bf16[2,14,1,16,128]{4,3,2,1,0:T(8,128)(2,1)S(1)}, f32[4,16,128]{2,1,0:T(8,128)S(1)}) custom-call(s32[2]{0:T(128)} %dil_h.1, bf16[4,16,128]{2,1,0:T(8,128)(2,1)} %bitcast.4, bf16[3,3,48,128]{3,2,1,0:T(8,128)(2,1)} %kern_h.1, f32[1,48]{1,0:T(1,128)} %bitcast.5, bf16[5,48]{1,0:T(8,128)(2,1)} %mix_h.1, ...), custom_call_target="tpu_custom_call" | custom-call | tf_op jit(solution)/shard_map/pallas_call | solution.py:726
  47.0 0.7 %shard_map.95 = (f32[5,32,64]{2,1,0:T(8,128)}, f32[27,16,128]{2,1,0:T(8,128)}, f32[4,16,128]{2,1,0:T(8,128)}) custom-call(f32[5,32,64]{2,1,0:T(8,128)S(1)} %get-tuple-element.9.contact, bf16[2,14,1,16,128]{4,3,2,1,0:T(8,128)(2,1)S(1)} %get-tuple-element.10.grad, f32[4,16,128]{2,1,0:T(8,128)S(1)} %get-tuple-element.11.emb), custom_call_target="tpu_custom_call" | custom-call | tf_op jit(solution)/shard_map/pallas_call | solution.py:751
